TPU v7x, 256 devices: a 2x2x32 block of a 4x8x32 slice. The times are simulated.
256 devices in a mesh: beam: 4 (over y, x), fft: 64 (over z, core).
Axes of the slice: x: 2, y: 2, z: 32, core: 2. Of those that a mesh axis runs over, the one named last changes fastest.
The devices are a block of a 4x8x32 slice.
Arguments:
- baseband: bfloat16 [8, 33554432], P('beam', 'fft'), parts along dimension 0, may hold values from -6 to 6
- spectrum_in: bfloat16 [8, 4096, 8192], P('beam', 'fft'), parts along dimension 0, may hold values from -6 to 6
- dm_index: int32 [1], replicated, may hold values from 0 to 63
Outputs:
- spectrum_out: bfloat16 [8, 4096, 8192], P('beam', 'fft'), parts along dimension 0
- smoothed: float32 [4, 2097152], P('beam', 'fft'), parts along dimension 0
There are 4 independent parts, one for each index of `beam`. A program takes and returns all parts, laid end to end along the dimension named above; an argument that names none is the same for every part. Nothing has to cross between parts.
Inputs may be any that keep to these rules, and one draw needn't show every extreme that they name: `dm_index`: indices into the grid of 64 trial dispersion measures.
All inputs are finite; a program needn't handle non-finite values.
Results may differ from a plain program's by a relative error of at most 0.0019.
The roundings to bfloat16 on the way count: a program that leaves them out, or rounds other values in their place, can miss the bound.
Values may be sent and summed in bfloat16 or wider, within the bound.
A program may use at most 64 MiB of HBM per device.

v0:
```python
import math

import jax
import jax.numpy as jnp
from jax import lax
from jax.sharding import Mesh
from jax.sharding import PartitionSpec as P

ROWS_OUTER = 32
ROWS_INNER = 128
COLS_OUTER = 64
COLS_INNER = 128
ROW_LENGTH = 4096
COLUMN_LENGTH = 8192
SEGMENT_SAMPLES = 33554432
DM_GRID = 64
DECIMATE_FACTOR = 16
HALF_WIDTH = 16
FFT = ("fft_0", "fft_1")


def cut_along(shard, dim, length):
    before, after = (shard.shape[:dim], shard.shape[dim + 1 :])
    return jnp.moveaxis(shard.reshape(*before, length, -1, *after), dim, 0)


def in_order(tiles, dim):
    lengths = list(tiles.shape[1:])
    lengths[dim] *= tiles.shape[0]
    return jnp.moveaxis(tiles, 0, dim).reshape(lengths)


def moved_by_axis(tiles, axes, turns):
    lengths = [lax.axis_size(a) for a in axes]
    tiles = tiles.reshape(*lengths, *tiles.shape[1:])
    for k in turns:
        tiles = lax.all_to_all(tiles, axes[k], split_axis=k, concat_axis=k, tiled=True)
    return tiles.reshape(-1, *tiles.shape[len(axes) :])


def exchange_by_chip(shard, groups, turns, split_dim, concat_dim):
    length = lax.axis_size(groups[0]) * lax.axis_size(groups[1])
    tiles = cut_along(shard, split_dim, length)
    return in_order(moved_by_axis(tiles, groups, turns), concat_dim)


def padded_2(block, sides, width):
    for axis, dim in sides:
        count = lax.axis_size(axis)
        forward = [(i, i + 1) for i in range(count - 1)]
        backward = [(target, source) for source, target in forward]
        low = lax.ppermute(
            lax.slice_in_dim(block, block.shape[dim] - width, None, axis=dim), axis, forward
        )
        high = lax.ppermute(lax.slice_in_dim(block, 0, width, axis=dim), axis, backward)
        block = jnp.concatenate([low, block, high], axis=dim)
    return block


def dft_table(length, direction):
    positions = jnp.arange(length, dtype=jnp.int32)
    product = jnp.remainder(positions[:, None] * positions[None, :], length)
    radians = direction * 2.0 * math.pi / length * product.astype(jnp.float32)
    norm_scale = 1.0 / math.sqrt(length)
    cosine = jnp.cos(radians) * norm_scale
    sine_part = jnp.sin(radians) * norm_scale
    return jnp.stack([jnp.stack([cosine, sine_part]), jnp.stack([-sine_part, cosine])]).astype(
        jnp.bfloat16
    )


def radians_of(numer, modulus, direction):
    return direction * 2.0 * math.pi / modulus * jnp.remainder(numer, modulus).astype(jnp.float32)


def chirp_radians(freq_row, col_outer, col_inner, grid_steps):
    col_freq = col_outer + COLS_OUTER * col_inner
    whole_mod = 4.0 * DM_GRID * ROW_LENGTH * COLUMN_LENGTH
    cross_mod = 2 * DM_GRID * COLUMN_LENGTH
    square_mod = 4 * DM_GRID * COLUMN_LENGTH
    grid_float = grid_steps.astype(jnp.float32)
    row_square = (freq_row * freq_row).astype(jnp.float32)
    term_rows = grid_float[:, None, None, None] * row_square[None, :, None, None] / whole_mod
    cross = jnp.remainder(freq_row[:, None, None] * col_freq[None], cross_mod)
    cross = jnp.remainder(grid_steps[:, None, None, None] * cross[None], cross_mod)
    square = jnp.remainder(col_freq * col_freq, square_mod)
    square = jnp.remainder(grid_steps[:, None, None] * square[None], square_mod)
    high_part = square // 512
    low_part = square % 512
    square = jnp.remainder(
        jnp.remainder(ROW_LENGTH * high_part, square_mod) * 512 + ROW_LENGTH * low_part, square_mod
    )
    turns = (
        term_rows
        + cross.astype(jnp.float32) / cross_mod
        + square[:, None].astype(jnp.float32) / square_mod
    )
    return 2.0 * math.pi * turns


def rotate(values, radians):
    cosine = jnp.cos(radians)
    sine_part = jnp.sin(radians)
    real_part = values[:, 0] * cosine - values[:, 1] * sine_part
    imag_part = values[:, 0] * sine_part + values[:, 1] * cosine
    return jnp.stack([real_part, imag_part], axis=1).astype(jnp.bfloat16)


def dft_section(values, einsum_form, length, direction, radians):
    mixed_sum = jnp.einsum(
        einsum_form, values, dft_table(length, direction), preferred_element_type=jnp.float32
    )
    if radians is None:
        return mixed_sum.astype(jnp.bfloat16)
    return rotate(mixed_sum, radians)


def row_frequency(row_pos):
    return row_pos // ROWS_INNER + ROWS_OUTER * (row_pos % ROWS_INNER)


def chirp_front(spectrum, grid_steps, row_start, row_local):
    trial_total = grid_steps.shape[0]
    row_pos = row_start + jnp.arange(row_local, dtype=jnp.int32)
    freq_row = row_frequency(row_pos)
    col_outer = jnp.arange(COLS_OUTER, dtype=jnp.int32)[:, None]
    col_inner = jnp.arange(COLS_INNER, dtype=jnp.int32)[None, :]
    values = rotate(
        spectrum.astype(jnp.float32).reshape(1, 2, row_local, COLS_OUTER, COLS_INNER),
        chirp_radians(freq_row, col_outer, col_inner, grid_steps),
    )
    values = dft_section(
        values,
        "dimjq,ioqy->domjy",
        COLS_INNER,
        1,
        radians_of(col_outer * col_inner, COLUMN_LENGTH, 1),
    )
    col_time = COLS_INNER * col_outer + col_inner
    values = dft_section(
        values,
        "dimjy,iojx->domxy",
        COLS_OUTER,
        1,
        radians_of(freq_row[:, None, None] * col_time[None], SEGMENT_SAMPLES, 1),
    )
    return values.reshape(trial_total, 2, row_local, COLUMN_LENGTH)


def finish_rows(values):
    trial_total = values.shape[0]
    col_local = values.shape[3]
    values = values.reshape(trial_total, 2, ROWS_OUTER, ROWS_INNER, col_local)
    outer_pos = jnp.arange(ROWS_OUTER, dtype=jnp.int32)[:, None]
    inner_pos = jnp.arange(ROWS_INNER, dtype=jnp.int32)[None, :]
    values = dft_section(
        values,
        "dikqb,ioqy->dokyb",
        ROWS_INNER,
        1,
        radians_of(outer_pos * inner_pos, ROW_LENGTH, 1)[:, :, None],
    )
    values = dft_section(values, "dikyb,iokx->doxyb", ROWS_OUTER, 1, None)
    return values.reshape(trial_total, 2, ROW_LENGTH, col_local)


def detect(values):
    trial_total = values.shape[0]
    row_total = values.shape[2]
    column_total = values.shape[3]
    wide = values.astype(jnp.float32)
    detected_power = wide[:, 0] * wide[:, 0] + wide[:, 1] * wide[:, 1]
    return jnp.mean(
        detected_power.reshape(
            trial_total, row_total, column_total // DECIMATE_FACTOR, DECIMATE_FACTOR
        ),
        axis=3,
    )


def on_device(baseband, spectrum_in, dm_index):
    device_index = lax.axis_index(FFT)
    row_local = spectrum_in.shape[1]
    col_local = COLUMN_LENGTH // (ROW_LENGTH // row_local)
    values = baseband.reshape(2, row_local, COLUMN_LENGTH)
    values = exchange_by_chip(values, ("fft_0", "fft_1"), (1, 0), 2, 1)
    values = values.reshape(1, 2, ROWS_OUTER, ROWS_INNER, col_local)
    outer_pos = jnp.arange(ROWS_OUTER, dtype=jnp.int32)[:, None]
    inner_pos = jnp.arange(ROWS_INNER, dtype=jnp.int32)[None, :]
    values = dft_section(
        values,
        "dixyb,ioxk->dokyb",
        ROWS_OUTER,
        -1,
        radians_of(outer_pos * inner_pos, ROW_LENGTH, -1)[:, :, None],
    )
    freq_row = outer_pos + ROWS_OUTER * inner_pos
    col_pos = device_index * col_local + jnp.arange(col_local, dtype=jnp.int32)
    values = dft_section(
        values,
        "dikyb,ioyq->dokqb",
        ROWS_INNER,
        -1,
        radians_of(freq_row[:, :, None] * col_pos[None, None, :], SEGMENT_SAMPLES, -1),
    )
    values = values.reshape(1, 2, ROW_LENGTH, col_local)
    values = exchange_by_chip(values, ("fft_0", "fft_1"), (1, 0), 2, 3)
    values = values.reshape(1, 2, row_local, COLS_OUTER, COLS_INNER)
    col_outer = jnp.arange(COLS_OUTER, dtype=jnp.int32)[:, None]
    col_inner = jnp.arange(COLS_INNER, dtype=jnp.int32)[None, :]
    values = dft_section(
        values,
        "dimxy,ioxj->domjy",
        COLS_OUTER,
        -1,
        radians_of(col_outer * col_inner, COLUMN_LENGTH, -1),
    )
    values = dft_section(values, "dimjy,ioyq->domjq", COLS_INNER, -1, None)
    spectrum_out = values[0].reshape(2, row_local, COLUMN_LENGTH)
    grid_steps = dm_index + 1
    row_start = device_index * row_local
    trial_total = dm_index.shape[0]
    front_part = chirp_front(spectrum_in, grid_steps, row_start, row_local)
    moved = exchange_by_chip(front_part, ("fft_0", "fft_1"), (1, 0), 3, 2)
    pieces = finish_rows(moved)
    decimated_power = lax.all_to_all(
        detect(pieces).astype(jnp.bfloat16), FFT, split_axis=1, concat_axis=2, tiled=True
    ).astype(jnp.float32)
    series = decimated_power.reshape(
        trial_total, decimated_power.shape[1] * decimated_power.shape[2]
    )
    padded = padded_2(series.astype(jnp.bfloat16), ((FFT, 1),), HALF_WIDTH).astype(series.dtype)
    length = series.shape[1]
    window_sum = padded[:, 0:length]
    for offset in range(1, 2 * HALF_WIDTH + 1):
        window_sum = window_sum + padded[:, offset : offset + length]
    smoothed = window_sum / (2 * HALF_WIDTH + 1)
    return (spectrum_out, smoothed)


def solution(mesh):
    torus = Mesh(mesh.devices.reshape(mesh.shape["beam"], 32, 2), ("beam", "fft_0", "fft_1"))
    return jax.shard_map(
        on_device,
        mesh=torus,
        in_specs=(P("beam", FFT), P("beam", FFT, None), P()),
        out_specs=(P("beam", FFT, None), P("beam", FFT)),
        check_vma=False,
    )
```

profile of v0, /device:TPU:46, one launch (start us, length us, event | category | flops | bytes accessed | tf_op | source)
XLA Modules:
  0.0 744.8 jit_solution(13776390596767978175)
XLA Ops:
  4.8 10.5 %fusion.37 = (bf16[1,64,64,128]{3,2,0,1:T(8,128)(2,1)S(1)}, bf16[1,64,64,128]{3,2,0,1:T(8,128)(2,1)S(1)}) fusion(f32[1,2,64,64,128]{4,3,2,1,0:T(8,128)S(1)} %bitcast.214, f32[64,128]{1,0:T(8,128)S(1)} %fusion.77, s32[64,128]{1,0:T(8,128)S(1)} %iota_add_fusion.1, s32[64]{0:T(128)S(1)} %fusion.103, s32[]{:T(128)} %bitcast.67, f32[64]{0:T(128)S(1)} %multiply_multiply_fusion), kind=kLoop, calls=%fused_computation.82 | loop fusion | flops 19398656 | bytes 6357508 | tf_op jit(solution)/shard_map/stack | solution.py:106
  17.4 9.4 %subtract_convert_fusion.1 = (bf16[1,1,64,64,128]{4,3,2,1,0:T(8,128)(2,1)S(1)}, bf16[1,1,64,64,128]{4,3,2,1,0:T(8,128)(2,1)S(1)}) fusion(f32[1,2,64,64,128]{4,3,2,1,0:T(8,128)S(1)} %convolution_bitcast_fusion.1, s32[64,128]{1,0:T(8,128)S(1)} %iota_add_fusion, s32[64]{0:T(128)S(1)} %fusion.103), kind=kLoop, calls=%fused_computation.65 | loop fusion | flops 11534336 | bytes 6324480 | tf_op jit(solution)/shard_map/convert.6
  28.7 3.8 all-to-all-start.4
  34.4 2.7 copy.143
  37.1 4.8 all-to-all-start
  41.9 3.5 copy.162
  45.4 33.1 %all-to-all-start.5 = ((bf16[32,2,1,2,64,128]{5,1,4,3,2,0:T(2,128)(2,1)}), bf16[32,2,1,2,64,128]{5,1,4,3,2,0:T(2,128)(2,1)S(1)}, u32[]{:S(2)}, u32[]{:S(2)}) async-start(bf16[32,2,1,2,64,128]{5,1,4,3,2,0:T(2,128)(2,1)} %copy.162), calls=%async_computation.5 | async-start | bytes 4194304 | tf_op jit(solution)/shard_map/all_to_all | solution.py:37
  78.5 3.2 copy.144
  81.7 188.3 %all-to-all-done.5 = bf16[32,2,1,2,64,128]{5,1,4,3,2,0:T(2,128)(2,1)S(1)} async-done(((bf16[32,2,1,2,64,128]{5,1,4,3,2,0:T(2,128)(2,1)}), bf16[32,2,1,2,64,128]{5,1,4,3,2,0:T(2,128)(2,1)S(1)}, u32[]{:S(2)}, u32[]{:S(2)}) %all-to-all-start.5) | async-done | bytes 2097184 | tf_op jit(solution)/shard_map/all_to_all | solution.py:37
  271.3 11.6 %all-to-all-start.1 = ((bf16[32,2,2,64,128]{4,3,1,2,0:T(8,128)(2,1)}), bf16[32,2,2,64,128]{4,3,1,2,0:T(8,128)(2,1)S(1)}, u32[]{:S(2)}, u32[]{:S(2)}) async-start(bf16[32,2,2,64,128]{4,3,1,2,0:T(8,128)(2,1)} %copy.144), calls=%async_computation.1 | async-start | bytes 4194304 | tf_op jit(solution)/shard_map/all_to_all | solution.py:37
  294.6 2.9 copy.169
  299.4 3.8 copy.170
  303.8 23.6 %reduce.2 = bf16[4096,8]{1,0:T(8,128)(2,1)S(1)} reduce(bf16[4096,1,8]{2,1,0:T(2,128)(2,1)} %bitcast.219, bf16[]{:T(256)} %broadcast.2052), dimensions={1}, to_apply=%bitcast.202.reduce_sub_computation | reduce | bytes 131074
  329.2 145.4 %all-to-all-done.1 = bf16[32,2,2,64,128]{4,3,1,2,0:T(8,128)(2,1)S(1)} async-done(((bf16[32,2,2,64,128]{4,3,1,2,0:T(8,128)(2,1)}), bf16[32,2,2,64,128]{4,3,1,2,0:T(8,128)(2,1)S(1)}, u32[]{:S(2)}, u32[]{:S(2)}) %all-to-all-start.1) | async-done | bytes 2097184 | tf_op jit(solution)/shard_map/all_to_all | solution.py:37
  479.0 9.6 %subtract_convert_fusion.5 = (bf16[1,1,32,128,128]{4,3,2,1,0:T(8,128)(2,1)S(1)}, bf16[1,1,32,128,128]{4,3,2,1,0:T(8,128)(2,1)S(1)}) fusion(f32[1,2,32,128,128]{4,3,2,1,0:T(8,128)S(1)} %convolution_bitcast_fusion.4, s32[128]{0:T(128)S(1)} %iota_add_fusion.3, s32[32,128]{1,0:T(8,128)S(1)} %iota_add_fusion.2), kind=kLoop, calls=%fused_computation.73 | loop fusion | flops 11534336 | bytes 6308352 | tf_op jit(solution)/shard_map/convert.47
  490.2 5.4 all_to_all.48
  495.7 12.5 %all-to-all-start.6 = ((bf16[64,2,256]{2,1,0:T(2,128)(2,1)}), bf16[64,2,256]{2,1,0:T(2,128)(2,1)S(1)}, u32[]{:S(2)}, u32[]{:S(2)}) async-start(bf16[64,2,256]{2,1,0:T(2,128)(2,1)} %reshape.1482), calls=%async_computation.6 | async-start | bytes 131072 | tf_op jit(solution)/shard_map/all_to_all | solution.py:226
  508.2 3.5 copy.153
  511.7 21.4 %all-to-all-done.6 = bf16[64,2,256]{2,1,0:T(2,128)(2,1)S(1)} async-done(((bf16[64,2,256]{2,1,0:T(2,128)(2,1)}), bf16[64,2,256]{2,1,0:T(2,128)(2,1)S(1)}, u32[]{:S(2)}, u32[]{:S(2)}) %all-to-all-start.6) | async-done | bytes 65568 | tf_op jit(solution)/shard_map/all_to_all | solution.py:226
  533.1 4.9 all-to-all-start.3
  539.7 4.5 reshape.1483
  544.3 4.4 copy.171
  557.7 9.6 %fusion.49 = f32[1,32768]{1,0:T(1,128)} fusion(f32[1,32800]{1,0:T(1,128)S(1)} %convert_element_type.399), kind=kLoop, calls=%fused_computation.95 | loop fusion | flops 1081344 | bytes 4456448 | tf_op jit(solution)/shard_map/div | solution.py:237
  567.3 170.2 %all-to-all-done.3 = bf16[32,2,1,2,64,128]{5,1,3,4,2,0:T(2,128)(2,1)S(1)} async-done(((bf16[32,2,1,2,64,128]{5,1,3,4,2,0:T(2,128)(2,1)}), bf16[32,2,1,2,64,128]{5,1,3,4,2,0:T(2,128)(2,1)S(1)}, u32[]{:S(2)}, u32[]{:S(2)}) %all-to-all-start.3) | async-done | bytes 2097184 | tf_op jit(solution)/shard_map/all_to_all | solution.py:37
  (89 shorter events, 49.8 us)
Async XLA Ops:
  28.7 8.3 %all-to-all-start.4 = ((bf16[32,2,1,2,64,128]{5,0,4,3,2,1:T(8,128)(2,1)}), bf16[32,2,1,2,64,128]{5,0,4,3,2,1:T(8,128)(2,1)S(1)}, u32[]{:S(2)}, u32[]{:S(2)}) async-start(bf16[32,2,1,2,64,128]{5,0,4,3,2,1:T(8,128)(2,1)} %copy.161), calls=%async_computation.4 | async-start | bytes 4194304 | tf_op jit(solution)/shard_map/all_to_all | solution.py:37
  37.1 8.3 %all-to-all-start = ((bf16[32,2,2,64,128]{4,3,0,2,1:T(8,128)(2,1)}), bf16[32,2,2,64,128]{4,3,0,2,1:T(8,128)(2,1)}, u32[]{:S(2)}, u32[]{:S(2)}) async-start(bf16[32,2,2,64,128]{4,3,0,2,1:T(8,128)(2,1)} %copy.143), calls=%async_computation | async-start | bytes 4194304 | tf_op jit(solution)/shard_map/all_to_all | solution.py:37
  45.4 224.6 %all-to-all-start.5 = ((bf16[32,2,1,2,64,128]{5,1,4,3,2,0:T(2,128)(2,1)}), bf16[32,2,1,2,64,128]{5,1,4,3,2,0:T(2,128)(2,1)S(1)}, u32[]{:S(2)}, u32[]{:S(2)}) async-start(bf16[32,2,1,2,64,128]{5,1,4,3,2,0:T(2,128)(2,1)} %copy.162), calls=%async_computation.5 | async-start | bytes 4194304 | tf_op jit(solution)/shard_map/all_to_all | solution.py:37
  270.0 1.3 copy-start
  271.3 203.2 %all-to-all-start.1 = ((bf16[32,2,2,64,128]{4,3,1,2,0:T(8,128)(2,1)}), bf16[32,2,2,64,128]{4,3,1,2,0:T(8,128)(2,1)S(1)}, u32[]{:S(2)}, u32[]{:S(2)}) async-start(bf16[32,2,2,64,128]{4,3,1,2,0:T(8,128)(2,1)} %copy.144), calls=%async_computation.1 | async-start | bytes 4194304 | tf_op jit(solution)/shard_map/all_to_all | solution.py:37
  495.7 37.4 %all-to-all-start.6 = ((bf16[64,2,256]{2,1,0:T(2,128)(2,1)}), bf16[64,2,256]{2,1,0:T(2,128)(2,1)S(1)}, u32[]{:S(2)}, u32[]{:S(2)}) async-start(bf16[64,2,256]{2,1,0:T(2,128)(2,1)} %reshape.1482), calls=%async_computation.6 | async-start | bytes 131072 | tf_op jit(solution)/shard_map/all_to_all | solution.py:226
  533.1 204.4 %all-to-all-start.3 = ((bf16[32,2,1,2,64,128]{5,1,3,4,2,0:T(2,128)(2,1)}), bf16[32,2,1,2,64,128]{5,1,3,4,2,0:T(2,128)(2,1)S(1)}, u32[]{:S(2)}, u32[]{:S(2)}) async-start(bf16[32,2,1,2,64,128]{5,1,3,4,2,0:T(2,128)(2,1)} %copy.153), calls=%async_computation.3 | async-start | bytes 4194304 | tf_op jit(solution)/shard_map/all_to_all | solution.py:37
  551.6 3.0 collective-permute-start
  553.3 4.0 collective-permute-start.1
  567.3 172.6 %copy-start.1 = (bf16[1,2,64,64]{2,3,0,1:T(8,128)(2,1)S(1)}, bf16[1,2,64,64]{2,3,0,1:T(8,128)(2,1)}, u32[]{:S(2)}) copy-start(bf16[1,2,64,64]{2,3,0,1:T(8,128)(2,1)} %get-tuple-element.24) | copy-start | bytes 49156
  567.3 172.6 %copy-start.2 = (bf16[1,2,64,64]{2,3,0,1:T(8,128)(2,1)S(1)}, bf16[1,2,64,64]{2,3,0,1:T(8,128)(2,1)}, u32[]{:S(2)}) copy-start(bf16[1,2,64,64]{2,3,0,1:T(8,128)(2,1)} %get-tuple-element.25) | copy-start | bytes 49156
  739.9 0.8 copy-start.3
  739.9 0.8 copy-start.4
where the time goes:
time: 754 us; the launch traced here: 745 us
  waiting for transfers between devices  525 us (70%)
  other arithmetic  75.6 us (10%)
  starting transfers between devices  73.8 us (10%)
  local copies, waits for them, and re-layouts  54.4 us (7%)
  matrix products  8.03 us (1%)
    all_to_all x5, waiting for transfers between devices, moved_by_axis(): lax.all_to_all(tiles, axes[k], split_axis=k, concat_axis=k, tiled=True)  504 us
    all_to_all x5, starting transfers between devices, moved_by_axis(): lax.all_to_all(tiles, axes[k], split_axis=k, concat_axis=k, tiled=True)  58.3 us
    unnamed x2, other arithmetic  23.6 us
    all_to_all x1, waiting for transfers between devices, on_device(): lax.all_to_all(detect(pieces).astype(jnp.bfloat16), FFT, split_axis=1, co...  21.4 us
    another operation x14, other arithmetic  21.1 us
    another operation x9, other arithmetic, rotate(): return jnp.stack([real_part, imag_part], axis=1).astype(jnp.bfloat16)  15.5 us
  transfers between devices with their start and end apart: 8, of which 4 were waited for; matrix products, arithmetic and copies ran while one was open for 12% of the time, Pallas kernels for 0%

commit v1 on v0

v1 whole, which is shorter than its diff:
```python
import functools
import math

import jax
import jax.numpy as jnp
import numpy as np
from jax import lax
from jax.experimental import pallas as pl
from jax.experimental.pallas import tpu as pltpu
from jax.sharding import PartitionSpec as P

ROWS_OUTER = 32
ROWS_INNER = 128
COLS_OUTER = 64
COLS_INNER = 128
ROW_LENGTH = 4096
COLUMN_LENGTH = 8192
SEGMENT_SAMPLES = 33554432
DM_GRID = 64
DECIMATE_FACTOR = 16
HALF_WIDTH = 16
LANES = 128
MESH = pl.DeviceIdType.MESH
F32 = jnp.float32
BF16 = jnp.bfloat16


def table(length, direction):
    product = np.outer(np.arange(length), np.arange(length)) % length
    radians = np.float32(direction * 2.0 * math.pi / length) * product.astype(np.float32)
    scale = np.float32(1.0 / math.sqrt(length))
    cosine = np.cos(radians).astype(np.float32) * scale
    sine = np.sin(radians).astype(np.float32) * scale
    return np.stack([np.stack([cosine, sine]), np.stack([-sine, cosine])])


def left_matrix(length, direction, parts_inner=False):
    t = table(length, direction).transpose(1, 3, 0, 2)
    if parts_inner:
        t = t.transpose(0, 1, 3, 2)
    return jnp.asarray(t.reshape(2 * length, 2 * length), BF16)


def right_matrix(length, direction):
    return jnp.asarray(table(length, direction).transpose(0, 2, 1, 3).reshape(2 * length, 2 * length), BF16)


def cos_sin(turns):
    quarter = jnp.round(turns * 4.0)
    theta = (turns - quarter * 0.25) * (2.0 * math.pi)
    z = theta * theta
    s = theta * (1.0 + z * (-1.0 / 6 + z * (1.0 / 120 + z * (-1.0 / 5040 + z * (1.0 / 362880)))))
    c = 1.0 + z * (-0.5 + z * (1.0 / 24 + z * (-1.0 / 720 + z * (1.0 / 40320))))
    q = quarter.astype(jnp.int32)
    odd = (q & 1) == 1
    cc = jnp.where(odd, s, c)
    ss = jnp.where(odd, c, s)
    cc = jnp.where(((q + 1) & 2) == 2, -cc, cc)
    ss = jnp.where((q & 2) == 2, -ss, ss)
    return cc, ss


def unit(numer, modulus):
    half = modulus // 2
    centred = ((numer + half) & (modulus - 1)) - half
    return cos_sin(centred.astype(F32) * (1.0 / modulus))


def iota(shape, dim):
    return lax.broadcasted_iota(jnp.int32, shape, dim)


def dot(a, b):
    return jnp.dot(a, b, preferred_element_type=F32)


def order(i, chips):
    t = chips - 1 - i
    odd = lax.rem(t, 2)
    return odd * lax.div(t + 1, 2) + (1 - odd) * (chips - lax.div(t, 2))


def kernel(
    n, rows, axis,
    dm_ref, xb, spec, m1f, m2f, m3f, m4f, m1i, m2i, m3i, m4i,
    out_ref, smooth_ref,
    spec_v, r1, r2, r3, s2, s3, fa, fb, sd, ra, rb, tb, halo, tpad, sm, twc, tws,
    send1, recv1, send2, recv2, send3, recv3, send_d, recv_d, misc,
):
    me = lax.axis_index(axis)
    chips = n // 2
    z = lax.div(me, 2)
    core = lax.rem(me, 2)

    def peer(i):
        dz = order(lax.div(i, 2), chips)
        dc = 1 - lax.rem(i, 2)
        return lax.rem(z + dz, chips) * 2 + lax.rem(core + dc, 2)

    load_spec = pltpu.make_async_copy(spec, spec_v, misc.at[0])
    load_spec.start()
    load_own = pltpu.make_async_copy(xb.at[me], r1.at[me], misc.at[1])
    load_own.start()

    barrier = pltpu.get_barrier_semaphore()

    @pl.loop(0, n - 1)
    def _(i):
        pl.semaphore_signal(barrier, inc=1, device_id={axis: peer(i)}, device_id_type=MESH)

    pl.semaphore_wait(barrier, n - 1)

    def remote(src, dst, send, recv, target):
        return pltpu.make_async_remote_copy(
            src_ref=src, dst_ref=dst, send_sem=send, recv_sem=recv,
            device_id={axis: target}, device_id_type=MESH,
        )

    def first(i):
        x = peer(i)
        return remote(xb.at[x], r1.at[me], send1.at[i], recv1.at[i], x)

    @pl.loop(0, n - 1)
    def _(i):
        first(i).start()

    m_iota = iota((rows, LANES), 0)
    lane = iota((rows, LANES), 1)
    freq_row = z + ROWS_OUTER * (rows * core + m_iota)
    steps = dm_ref[0] + 1
    row_turns = (steps * freq_row * freq_row).astype(F32) * (2.0 ** -33)
    load_spec.wait()

    @pl.loop(0, COLS_OUTER)
    def _(c):
        at = pl.ds(pl.multiple_of(c * LANES, LANES), LANES)
        re = spec_v[0, :, at].astype(F32)
        im = spec_v[1, :, at].astype(F32)
        col = c + COLS_OUTER * lane
        cross = (steps * (freq_row * col)) & (2 * DM_GRID * COLUMN_LENGTH - 1)
        square = (steps * ((col * col) & 511)) & 511
        turns = row_turns + cross.astype(F32) * (0.5 / (DM_GRID * COLUMN_LENGTH)) + square.astype(F32) * (1.0 / 512)
        co, si = cos_sin(turns)
        a = jnp.concatenate([(re * co - im * si).astype(BF16), (re * si + im * co).astype(BF16)], axis=1)
        w = dot(a, m4i[...])
        wr, wi = w[:, :LANES], w[:, LANES:]
        co, si = unit(c * lane, COLUMN_LENGTH)
        fa[pl.ds(pl.multiple_of(c * rows, rows), rows), :] = wr * co - wi * si
        fa[pl.ds(pl.multiple_of((COLS_OUTER + c) * rows, rows), rows), :] = wr * si + wi * co

    half = iota((COLS_OUTER, LANES), 0)
    half_lane = iota((COLS_OUTER, LANES), 1)

    @pl.loop(0, rows)
    def _(m):
        x = fa[pl.ds(m, 2 * COLS_OUTER, stride=rows), :].astype(BF16)
        w = dot(m3i[...], x)
        wr, wi = w[:COLS_OUTER], w[COLS_OUTER:]
        k = z + ROWS_OUTER * (rows * core + m)
        co, si = unit((LANES * half + half_lane) * k, SEGMENT_SAMPLES)
        fb[pl.ds(m, COLS_OUTER, stride=2 * rows), :] = wr * co - wi * si
        fb[pl.ds(rows + m, COLS_OUTER, stride=2 * rows), :] = wr * si + wi * co

    def second(i):
        x = peer(i)
        return remote(s2.at[x], r2.at[me], send2.at[i], recv2.at[i], x)

    @pl.loop(0, n - 1)
    def _(i):
        x = peer(i)
        s2[x] = fb[pl.ds(pl.multiple_of(x * 2 * rows, 2 * rows), 2 * rows), :].astype(BF16)
        second(i).start()

    r2[me] = fb[pl.ds(pl.multiple_of(me * 2 * rows, 2 * rows), 2 * rows), :].astype(BF16)

    load_own.wait()

    @pl.loop(0, n - 1)
    def _(i):
        first(i).wait_recv()

    @pl.loop(0, n)
    def _(d):
        fa[pl.ds(pl.multiple_of(d * 2 * rows, 2 * rows), 2 * rows), :] = r1[d].astype(F32)

    p_iota = iota((ROWS_OUTER, LANES), 0)

    @pl.loop(0, rows)
    def _(j):
        def columns(g):
            start = g * 2 * rows + j
            parts = [fa[pl.ds(start + part * rows, ROWS_OUTER, stride=4 * rows), :] for part in range(2)]
            return jnp.concatenate(parts, axis=0).astype(BF16)

        u = dot(m1f[...], jnp.concatenate([columns(0), columns(1)], axis=1))
        for g in range(2):
            n2 = g * rows + j
            ur = u[:ROWS_OUTER, g * LANES : (g + 1) * LANES]
            ui = u[ROWS_OUTER:, g * LANES : (g + 1) * LANES]
            co, si = unit(p_iota * n2, ROW_LENGTH)
            fb[pl.ds(n2, ROWS_OUTER, stride=ROWS_INNER), :] = ur * co + ui * si
            fb[pl.ds(ROW_LENGTH + n2, ROWS_OUTER, stride=ROWS_INNER), :] = ui * co - ur * si

    q_iota = iota((ROWS_INNER, LANES), 0)
    q_lane = iota((ROWS_INNER, LANES), 1)

    def third(i):
        x = peer(i)
        return remote(s3.at[x], r3.at[me], send3.at[i], recv3.at[i], x)

    @pl.loop(0, chips)
    def _(i):
        p = lax.rem(z + order(i, chips), chips)
        at = pl.multiple_of(p * ROWS_INNER, ROWS_INNER)
        x = jnp.concatenate(
            [fb[pl.ds(at, ROWS_INNER), :].astype(BF16), fb[pl.ds(ROW_LENGTH + at, ROWS_INNER), :].astype(BF16)], axis=0
        )
        u = dot(m2f[...], x)
        ur, ui = u[:ROWS_INNER], u[ROWS_INNER:]
        co, si = unit((LANES * me + q_lane) * (p + ROWS_OUTER * q_iota), SEGMENT_SAMPLES)
        re = (ur * co + ui * si).astype(BF16)
        im = (ui * co - ur * si).astype(BF16)
        for h in range(2):
            s3[2 * p + h, :rows, :] = re[h * rows : (h + 1) * rows]
            s3[2 * p + h, rows:, :] = im[h * rows : (h + 1) * rows]
        third(2 * i).start()

        @pl.when(i < chips - 1)
        def _():
            third(2 * i + 1).start()

    r3[me] = s3[me]

    @pl.loop(0, n - 1)
    def _(i):
        second(i).wait_recv()

    @pl.loop(0, chips)
    def _(p):
        x = jnp.concatenate(
            [r2[2 * p, :rows, :], r2[2 * p + 1, :rows, :], r2[2 * p, rows:, :], r2[2 * p + 1, rows:, :]], axis=0
        )
        w = dot(m2i[...], x)
        wr, wi = w[:ROWS_INNER], w[ROWS_INNER:]
        co, si = unit(p * q_iota, ROW_LENGTH)
        at = pl.multiple_of(p * ROWS_INNER, ROWS_INNER)
        fa[pl.ds(at, ROWS_INNER), :] = wr * co - wi * si
        fa[pl.ds(ROW_LENGTH + at, ROWS_INNER), :] = wr * si + wi * co

    @pl.loop(0, rows)
    def _(j):
        x = jnp.concatenate(
            [fa[pl.ds(g * rows + j, 2 * ROWS_OUTER, stride=ROWS_INNER), :].astype(BF16) for g in range(2)], axis=1
        )
        w = dot(m1i[...], x).astype(BF16).astype(F32)
        power = w[:ROWS_OUTER] * w[:ROWS_OUTER] + w[ROWS_OUTER:] * w[ROWS_OUTER:]
        for g in range(2):
            fb[pl.ds(g * rows + j, ROWS_OUTER, stride=ROWS_INNER), :] = power[:, g * LANES : (g + 1) * LANES]

    groups = LANES // DECIMATE_FACTOR
    mean = (iota((groups, LANES), 1) // DECIMATE_FACTOR == iota((groups, LANES), 0)).astype(F32).astype(BF16)

    def averaged(at):
        power = fb[pl.ds(pl.multiple_of(at * ROWS_INNER, ROWS_INNER), ROWS_INNER), :]
        high = power.astype(BF16)
        low = (power - high.astype(F32)).astype(BF16)
        total = sum(
            lax.dot_general(mean, part, (((1,), (1,)), ((), ())), preferred_element_type=F32) for part in (high, low)
        )
        return (total * (1.0 / DECIMATE_FACTOR)).astype(BF16)

    def detected(i):
        x = lax.rem(z + order(i, chips), chips)
        return remote(sd.at[x], ra.at[z], send_d.at[i], recv_d.at[i], 2 * x + core)

    @pl.loop(0, chips - 1)
    def _(i):
        x = lax.rem(z + order(i, chips), chips)
        sd[x] = averaged(x)
        detected(i).start()

    ra[z] = averaged(z)

    @pl.loop(0, chips - 1)
    def _(i):
        detected(i).wait_recv()

    swap = remote(ra, rb, misc.at[2], misc.at[3], 2 * z + 1 - core)
    swap.start()
    swap.wait_recv()

    @pl.loop(0, chips)
    def _(i):
        own = pl.multiple_of(groups * (2 * i + core), groups)
        other = pl.multiple_of(groups * (2 * i + 1 - core), groups)
        tpad[pl.ds(HALF_WIDTH + own, groups), :] = ra[i].astype(F32)
        tpad[pl.ds(HALF_WIDTH + other, groups), :] = rb[i].astype(F32)

    series = groups * n
    tb[0] = tpad[HALF_WIDTH : 2 * HALF_WIDTH, :].astype(BF16)
    tb[1] = tpad[series : series + HALF_WIDTH, :].astype(BF16)
    aside = lax.rem(z + core + (1 - core) * (chips - 1), chips)
    edge = remote(tb.at[core], halo, misc.at[4], misc.at[5], 2 * aside + 1 - core)
    edge.start()
    edge.wait_recv()
    inside = ((z > 0) | (core == 1)) & ((z < chips - 1) | (core == 0))
    got = jnp.where(inside, halo[...].astype(F32), 0.0)
    edge_lane = iota((HALF_WIDTH, LANES), 1)
    above = jnp.where(edge_lane == 0, pltpu.roll(got, 1, 1), pltpu.roll(tpad[series : series + HALF_WIDTH, :], 1, 1))
    below = jnp.where(
        edge_lane == LANES - 1,
        pltpu.roll(got, LANES - 1, 1),
        pltpu.roll(tpad[HALF_WIDTH : 2 * HALF_WIDTH, :], LANES - 1, 1),
    )
    tpad[:HALF_WIDTH, :] = above
    tpad[series + HALF_WIDTH :, :] = below
    width = 2 * HALF_WIDTH

    @pl.loop(0, series // LANES)
    def _(i):
        at = pl.multiple_of(i * LANES, LANES)
        offset = iota((LANES, LANES + width), 1) - iota((LANES, LANES + width), 0)
        band = jnp.where((offset >= 0) & (offset <= width), 1.0, 0.0).astype(BF16)
        total = dot(band, tpad[pl.ds(at, LANES + width), :].astype(BF16))
        sm[:, pl.ds(at, LANES)] = total.T / (width + 1.0)

    smooth_ref[...] = sm[pl.ds(pl.multiple_of(core * rows, rows), rows), :]

    co, si = unit(half * half_lane, COLUMN_LENGTH)
    twc[...] = co
    tws[...] = si

    @pl.loop(0, n - 1)
    def _(i):
        third(i).wait_recv()

    @pl.loop(0, n)
    def _(d):
        fa[pl.ds(pl.multiple_of(d * 2 * rows, 2 * rows), 2 * rows), :] = r3[d].astype(F32)

    @pl.loop(0, rows)
    def _(m):
        x = fa[pl.ds(m, 2 * n, stride=rows), :].astype(BF16)
        v = dot(m3f[...], x)
        vr, vi = v[:COLS_OUTER], v[COLS_OUTER:]
        co, si = twc[...], tws[...]
        fb[pl.ds(m, COLS_OUTER, stride=rows), :] = vr * co + vi * si
        fb[pl.ds(COLS_OUTER * rows + m, COLS_OUTER, stride=rows), :] = vi * co - vr * si

    @pl.loop(0, COLS_OUTER)
    def _(c):
        at = pl.multiple_of(c * rows, rows)
        a = jnp.concatenate(
            [fb[pl.ds(at, rows), :].astype(BF16), fb[pl.ds(COLS_OUTER * rows + at, rows), :].astype(BF16)], axis=1
        )
        v = dot(a, m4f[...]).astype(BF16)
        lanes = pl.ds(pl.multiple_of(c * LANES, LANES), LANES)
        out_ref[0, :, lanes] = v[:, :LANES]
        out_ref[1, :, lanes] = v[:, LANES:]

    @pl.loop(0, n - 1)
    def _(i):
        first(i).wait_send()
        second(i).wait_send()
        third(i).wait_send()

    @pl.loop(0, chips - 1)
    def _(i):
        detected(i).wait_send()

    swap.wait_send()
    edge.wait_send()


def on_device(n, baseband, spectrum_in, dm_index):
    rows = spectrum_in.shape[1]
    chips = n // 2
    assert (rows * n, chips, n) == (ROW_LENGTH, ROWS_OUTER, COLS_OUTER)
    groups = LANES // DECIMATE_FACTOR
    blocks = baseband.reshape(2, rows, n, LANES).transpose(2, 0, 1, 3).reshape(n, 2 * rows, LANES)
    matrices = (
        left_matrix(ROWS_OUTER, -1), left_matrix(ROWS_INNER, -1),
        left_matrix(COLS_OUTER, -1, True), right_matrix(COLS_INNER, -1),
        left_matrix(ROWS_OUTER, 1), left_matrix(ROWS_INNER, 1),
        left_matrix(COLS_OUTER, 1), right_matrix(COLS_INNER, 1),
    )
    block = pltpu.VMEM((n, 2 * rows, LANES), BF16)
    floats = pltpu.VMEM((n * 2 * rows, LANES), F32)
    dma = pltpu.SemaphoreType.DMA
    anywhere = pl.BlockSpec(memory_space=pl.ANY)
    vmem = pl.BlockSpec(memory_space=pltpu.VMEM)
    spectrum_out, smoothed = pl.pallas_call(
        functools.partial(kernel, n, rows, "fft"),
        out_shape=(
            jax.ShapeDtypeStruct(spectrum_in.shape, BF16),
            jax.ShapeDtypeStruct((rows, groups * n), F32),
        ),
        in_specs=[pl.BlockSpec(memory_space=pltpu.SMEM), anywhere, anywhere] + [vmem] * 8,
        out_specs=(vmem, vmem),
        scratch_shapes=[
            pltpu.VMEM(spectrum_in.shape, BF16), block, block, block, block, block, floats, floats,
            pltpu.VMEM((chips, groups, LANES), BF16), pltpu.VMEM((chips, groups, LANES), BF16),
            pltpu.VMEM((chips, groups, LANES), BF16), pltpu.VMEM((2, HALF_WIDTH, LANES), BF16),
            pltpu.VMEM((HALF_WIDTH, LANES), BF16), pltpu.VMEM((groups * n + 2 * HALF_WIDTH, LANES), F32),
            pltpu.VMEM((LANES, groups * n), F32),
            pltpu.VMEM((COLS_OUTER, LANES), F32), pltpu.VMEM((COLS_OUTER, LANES), F32),
            dma((n,)), dma((n,)), dma((n,)), dma((n,)), dma((n,)), dma((n,)), dma((chips,)), dma((chips,)), dma((6,)),
        ],
        compiler_params=pltpu.CompilerParams(
            collective_id=0, has_side_effects=True, vmem_limit_bytes=60 * 2**20
        ),
        name="dedisperse",
    )(dm_index, blocks, spectrum_in, *matrices)
    return spectrum_out, smoothed.reshape(1, -1)


def solution(mesh):
    return jax.shard_map(
        functools.partial(on_device, mesh.shape["fft"]),
        mesh=mesh,
        in_specs=(P("beam", "fft"), P("beam", "fft", None), P()),
        out_specs=(P("beam", "fft", None), P("beam", "fft")),
        check_vma=False,
    )
```

time: 754 us -> 634 us (0.84); the launches traced: 745 us -> 634 us
  Pallas kernels: 0 us -> 624 us
  waiting for transfers between devices: 525 us -> 0 us
  other arithmetic: 75.6 us -> 0 us
  starting transfers between devices: 73.8 us -> 0 us
  local copies, waits for them, and re-layouts: 54.4 us -> 9.32 us
  matrix products: 8.03 us -> 0 us
    pallas_call x0 -> x1, Pallas kernels: none -> 624 us  [on_device(): pl.pallas_call(functools.partial(kernel, n, rows, 'fft'), out_shape=(jax....]
    all_to_all x6 -> x0, waiting for transfers between devices: 525 us -> none  [the longest x5 504 us: moved_by_axis(): lax.all_to_all(tiles, axes[k], split_axis=k, concat_axis=k, tiled=True)]
    all_to_all x6 -> x0, starting transfers between devices: 70.8 us -> none  [the longest x5 58.3 us: moved_by_axis(): lax.all_to_all(tiles, axes[k], split_axis=k, concat_axis=k, tiled=True)]
    another operation x29 -> x0, other arithmetic: 37.3 us -> none
    unnamed x2 -> x0, other arithmetic: 23.6 us -> none
    all_to_all x8 -> x0, local copies, waits for them, and re-layouts: 19.7 us -> none  [the longest x4 12.5 us: moved_by_axis(): lax.all_to_all(tiles, axes[k], split_axis=k, concat_axis=k, tiled=True)]
    div x3 -> x0, other arithmetic: 9.71 us -> none  [the longest x1 9.59 us: on_device(): smoothed = window_sum / (2 * HALF_WIDTH + 1)]
    unnamed x17 -> x3, local copies, waits for them, and re-layouts: 14.9 us -> 6.65 us
  transfers between devices with their start and end apart: 8 -> 0, of which waited for: 4 -> 0; matrix products, arithmetic and copies ran while one was open for 12% -> 0% of each run, Pallas kernels for 0% -> 0%
where the time goes in v1:
time: 634 us
  Pallas kernels  624 us (98%)
  local copies, waits for them, and re-layouts  9.32 us (1%)
    pallas_call x1, Pallas kernels, on_device(): pl.pallas_call(functools.partial(kernel, n, rows, 'fft'), out_shape=(jax....  624 us

profile of v1, /device:TPU:46, one launch (start us, length us, event | category | flops | bytes accessed | tf_op | source)
XLA Modules:
  0.0 634.3 jit_solution(12747006395073790788)
XLA Ops:
  1.3 1.9 copy.14
  3.1 2.7 copy.13
  5.8 623.7 %dedisperse.1 = (bf16[2,64,8192]{2,1,0:T(8,128)(2,1)}, f32[64,512]{1,0:T(8,128)}) custom-call(s32[1]{0:T(128)S(6)} %copy.17.dm_ref, bf16[64,128,128]{2,1,0:T(8,128)(2,1)} %bitcast.9, bf16[2,64,8192]{2,1,0:T(8,128)(2,1)} %spec.1, bf16[64,64]{1,0:T(8,128)(2,1)} %constant.12.clone.m1f, bf16[256,256]{1,0:T(8,128)(2,1)} %constant.13.clone.m2f.m4i, ...), custom_call_target="tpu_custom_call" | custom-call | tf_op jit(solution)/shard_map/dedisperse/pallas_call | solution.py:392
  629.5 1.7 copy.15
  631.2 3.1 copy.18

commit v2 on v1

--- a/solution.py
+++ b/solution.py
@@ -21,6 +21,7 @@
 HALF_WIDTH = 16
 LANES = 128
 MESH = pl.DeviceIdType.MESH
+BATCHES = ((0, 4), (4, 2), (6, 1), (7, 1))
 F32 = jnp.float32
 BF16 = jnp.bfloat16
 
@@ -34,11 +35,8 @@
     return np.stack([np.stack([cosine, sine]), np.stack([-sine, cosine])])
 
 
-def left_matrix(length, direction, parts_inner=False):
-    t = table(length, direction).transpose(1, 3, 0, 2)
-    if parts_inner:
-        t = t.transpose(0, 1, 3, 2)
-    return jnp.asarray(t.reshape(2 * length, 2 * length), BF16)
+def left_matrix(length, direction):
+    return jnp.asarray(table(length, direction).transpose(1, 3, 0, 2).reshape(2 * length, 2 * length), BF16)
 
 
 def right_matrix(length, direction):
@@ -82,10 +80,10 @@
 
 def kernel(
     n, rows, axis,
-    dm_ref, xb, spec, m1f, m2f, m3f, m4f, m1i, m2i, m3i, m4i,
+    dm_ref, xb, spec, h1f, h2f, h3f, h4f, h1i, h2i, h3i, h4i,
     out_ref, smooth_ref,
-    spec_v, r1, r2, r3, s2, s3, fa, fb, sd, ra, rb, tb, halo, tpad, sm, twc, tws,
-    send1, recv1, send2, recv2, send3, recv3, send_d, recv_d, misc,
+    m1f, m2f, m3f, m4f, m1i, m2i, m3i, m4i, spec_v, r1, r2, r3, s2, s3, fa, fb, sd, ra, rb, tb, halo, tpad, sm, twc, tws,
+    send1, recv1, send2, recv2, send3, recv3, send_d, recv_d, misc, loaded, ready,
 ):
     me = lax.axis_index(axis)
     chips = n // 2
@@ -98,17 +96,22 @@
         return lax.rem(z + dz, chips) * 2 + lax.rem(core + dc, 2)
 
     load_spec = pltpu.make_async_copy(spec, spec_v, misc.at[0])
-    load_spec.start()
-    load_own = pltpu.make_async_copy(xb.at[me], r1.at[me], misc.at[1])
+    load_own = pltpu.make_async_copy(xb.at[:, me], r1.at[me], misc.at[1])
+    pairs = zip((h1f, h2f, h3f, h4f, h1i, h2i, h3i, h4i), (m1f, m2f, m3f, m4f, m1i, m2i, m3i, m4i))
+    loads = [load_spec] + [pltpu.make_async_copy(h, m, loaded.at[i]) for i, (h, m) in enumerate(pairs)]
+    for load in loads:
+        load.start()
     load_own.start()
 
     barrier = pltpu.get_barrier_semaphore()
 
-    @pl.loop(0, n - 1)
+    near, middle = 2 * (chips - 1 - chips // 4), 2 * (chips - 1 - chips // 2)
+
+    @pl.loop(near, n - 1)
     def _(i):
         pl.semaphore_signal(barrier, inc=1, device_id={axis: peer(i)}, device_id_type=MESH)
 
-    pl.semaphore_wait(barrier, n - 1)
+    pl.semaphore_wait(barrier, n - 1 - near)
 
     def remote(src, dst, send, recv, target):
         return pltpu.make_async_remote_copy(
@@ -118,18 +121,28 @@
 
     def first(i):
         x = peer(i)
-        return remote(xb.at[x], r1.at[me], send1.at[i], recv1.at[i], x)
-
-    @pl.loop(0, n - 1)
-    def _(i):
-        first(i).start()
+        return remote(xb.at[:, x], r1.at[me], send1.at[i], recv1.at[i], x)
+
+    def send_first(start, stop):
+        @pl.loop(start, stop)
+        def _(i):
+            first(i).start()
+
+    send_first(near, n - 1)
+    for level, (reach, start, stop) in enumerate(((chips // 8, middle, near), (chips // 4, 0, middle))):
+        for side in (reach, chips - reach):
+            target = 2 * lax.rem(z + side, chips) + core
+            pl.semaphore_signal(ready.at[level], inc=1, device_id={axis: target}, device_id_type=MESH)
+        pl.semaphore_wait(ready.at[level], 2)
+        send_first(start, stop)
 
     m_iota = iota((rows, LANES), 0)
     lane = iota((rows, LANES), 1)
     freq_row = z + ROWS_OUTER * (rows * core + m_iota)
     steps = dm_ref[0] + 1
     row_turns = (steps * freq_row * freq_row).astype(F32) * (2.0 ** -33)
-    load_spec.wait()
+    for load in loads:
+        load.wait()
 
     @pl.loop(0, COLS_OUTER)
     def _(c):
@@ -181,15 +194,15 @@
 
     @pl.loop(0, n)
     def _(d):
-        fa[pl.ds(pl.multiple_of(d * 2 * rows, 2 * rows), 2 * rows), :] = r1[d].astype(F32)
+        fa[pl.ds(pl.multiple_of(d * 2 * rows, 2 * rows), 2 * rows), :] = r1[d].astype(F32).reshape(2 * rows, LANES)
 
     p_iota = iota((ROWS_OUTER, LANES), 0)
 
     @pl.loop(0, rows)
     def _(j):
         def columns(g):
-            start = g * 2 * rows + j
-            parts = [fa[pl.ds(start + part * rows, ROWS_OUTER, stride=4 * rows), :] for part in range(2)]
+            start = g * 2 * rows + 2 * j
+            parts = [fa[pl.ds(start + part, ROWS_OUTER, stride=4 * rows), :] for part in range(2)]
             return jnp.concatenate(parts, axis=0).astype(BF16)
 
         u = dot(m1f[...], jnp.concatenate([columns(0), columns(1)], axis=1))
@@ -204,9 +217,12 @@
     q_iota = iota((ROWS_INNER, LANES), 0)
     q_lane = iota((ROWS_INNER, LANES), 1)
 
-    def third(i):
+    def third(batch, i):
         x = peer(i)
-        return remote(s3.at[x], r3.at[me], send3.at[i], recv3.at[i], x)
+        first_group, count = BATCHES[batch]
+        at = pl.ds(16 * first_group, 16 * count)
+        step = batch * n + i
+        return remote(s3.at[x, at], r3.at[me, at], send3.at[step], recv3.at[step], x)
 
     @pl.loop(0, chips)
     def _(i):
@@ -218,16 +234,16 @@
         u = dot(m2f[...], x)
         ur, ui = u[:ROWS_INNER], u[ROWS_INNER:]
         co, si = unit((LANES * me + q_lane) * (p + ROWS_OUTER * q_iota), SEGMENT_SAMPLES)
-        re = (ur * co + ui * si).astype(BF16)
-        im = (ui * co - ur * si).astype(BF16)
-        for h in range(2):
-            s3[2 * p + h, :rows, :] = re[h * rows : (h + 1) * rows]
-            s3[2 * p + h, rows:, :] = im[h * rows : (h + 1) * rows]
-        third(2 * i).start()
+        re = (ur * co + ui * si).reshape(2 * rows // 8, 1, 8, LANES)
+        im = (ui * co - ur * si).reshape(2 * rows // 8, 1, 8, LANES)
+        both = jnp.concatenate([re, im], axis=1).reshape(4 * rows, LANES).astype(BF16)
+        s3[2 * p] = both[: 2 * rows]
+        s3[2 * p + 1] = both[2 * rows :]
+        third(0, 2 * i).start()
 
         @pl.when(i < chips - 1)
         def _():
-            third(2 * i + 1).start()
+            third(0, 2 * i + 1).start()
 
     r3[me] = s3[me]
 
@@ -279,7 +295,48 @@
         sd[x] = averaged(x)
         detected(i).start()
 
+    def send_batch(batch):
+        @pl.loop(0, n - 1)
+        def _(i):
+            third(batch, i).start()
+
+    send_batch(1)
     ra[z] = averaged(z)
+
+    co, si = unit(half * half_lane, COLUMN_LENGTH)
+    twc[...] = co
+    tws[...] = si
+
+    def columns_of(batch):
+        @pl.loop(0, n - 1)
+        def _(i):
+            third(batch, i).wait_recv()
+
+        first_group, count = BATCHES[batch]
+
+        @pl.loop(first_group, first_group + count)
+        def _(g):
+            at = pl.ds(pl.multiple_of(16 * g, 16), 16)
+            for d in range(n):
+                fa[16 * d : 16 * (d + 1), :] = r3[d, at, :].astype(F32)
+            co, si = twc[...], tws[...]
+            for m in range(8):
+                x = jnp.concatenate([fa[pl.ds(8 * part + m, n, stride=16), :] for part in range(2)], axis=0)
+                v = dot(m3f[...], x.astype(BF16))
+                vr, vi = v[:COLS_OUTER], v[COLS_OUTER:]
+                fb[pl.ds(m, COLS_OUTER, stride=8), :] = vr * co + vi * si
+                fb[pl.ds(8 * COLS_OUTER + m, COLS_OUTER, stride=8), :] = vi * co - vr * si
+            a = jnp.concatenate(
+                [fb[: 8 * COLS_OUTER, :].astype(BF16), fb[8 * COLS_OUTER : 16 * COLS_OUTER, :].astype(BF16)], axis=1
+            )
+            v = dot(a, m4f[...])
+            at = pl.ds(pl.multiple_of(8 * g, 8), 8)
+            for c in range(COLS_OUTER):
+                for part in range(2):
+                    block = v[8 * c : 8 * (c + 1), part * LANES : (part + 1) * LANES]
+                    out_ref[part, at, c * LANES : (c + 1) * LANES] = block.astype(BF16)
+
+    columns_of(0)
 
     @pl.loop(0, chips - 1)
     def _(i):
@@ -302,6 +359,9 @@
     aside = lax.rem(z + core + (1 - core) * (chips - 1), chips)
     edge = remote(tb.at[core], halo, misc.at[4], misc.at[5], 2 * aside + 1 - core)
     edge.start()
+    for batch in range(2, len(BATCHES)):
+        send_batch(batch)
+    columns_of(1)
     edge.wait_recv()
     inside = ((z > 0) | (core == 1)) & ((z < chips - 1) | (core == 0))
     got = jnp.where(inside, halo[...].astype(F32), 0.0)
@@ -324,45 +384,19 @@
         total = dot(band, tpad[pl.ds(at, LANES + width), :].astype(BF16))
         sm[:, pl.ds(at, LANES)] = total.T / (width + 1.0)
 
-    smooth_ref[...] = sm[pl.ds(pl.multiple_of(core * rows, rows), rows), :]
-
-    co, si = unit(half * half_lane, COLUMN_LENGTH)
-    twc[...] = co
-    tws[...] = si
-
-    @pl.loop(0, n - 1)
-    def _(i):
-        third(i).wait_recv()
-
-    @pl.loop(0, n)
-    def _(d):
-        fa[pl.ds(pl.multiple_of(d * 2 * rows, 2 * rows), 2 * rows), :] = r3[d].astype(F32)
-
-    @pl.loop(0, rows)
-    def _(m):
-        x = fa[pl.ds(m, 2 * n, stride=rows), :].astype(BF16)
-        v = dot(m3f[...], x)
-        vr, vi = v[:COLS_OUTER], v[COLS_OUTER:]
-        co, si = twc[...], tws[...]
-        fb[pl.ds(m, COLS_OUTER, stride=rows), :] = vr * co + vi * si
-        fb[pl.ds(COLS_OUTER * rows + m, COLS_OUTER, stride=rows), :] = vi * co - vr * si
-
-    @pl.loop(0, COLS_OUTER)
-    def _(c):
-        at = pl.multiple_of(c * rows, rows)
-        a = jnp.concatenate(
-            [fb[pl.ds(at, rows), :].astype(BF16), fb[pl.ds(COLS_OUTER * rows + at, rows), :].astype(BF16)], axis=1
-        )
-        v = dot(a, m4f[...]).astype(BF16)
-        lanes = pl.ds(pl.multiple_of(c * LANES, LANES), LANES)
-        out_ref[0, :, lanes] = v[:, :LANES]
-        out_ref[1, :, lanes] = v[:, LANES:]
+    own_rows = pl.ds(pl.multiple_of(core * rows, rows), rows)
+    for i in range(series // LANES):
+        smooth_ref[pl.ds(i, rows, stride=series // LANES), :] = sm[own_rows, i * LANES : (i + 1) * LANES]
+
+    for batch in range(2, len(BATCHES)):
+        columns_of(batch)
 
     @pl.loop(0, n - 1)
     def _(i):
         first(i).wait_send()
         second(i).wait_send()
-        third(i).wait_send()
+        for batch in range(len(BATCHES)):
+            third(batch, i).wait_send()
 
     @pl.loop(0, chips - 1)
     def _(i):
@@ -377,40 +411,41 @@
     chips = n // 2
     assert (rows * n, chips, n) == (ROW_LENGTH, ROWS_OUTER, COLS_OUTER)
     groups = LANES // DECIMATE_FACTOR
-    blocks = baseband.reshape(2, rows, n, LANES).transpose(2, 0, 1, 3).reshape(n, 2 * rows, LANES)
+    blocks = baseband.reshape(2, rows, n, LANES).transpose(1, 2, 0, 3)
     matrices = (
         left_matrix(ROWS_OUTER, -1), left_matrix(ROWS_INNER, -1),
-        left_matrix(COLS_OUTER, -1, True), right_matrix(COLS_INNER, -1),
+        left_matrix(COLS_OUTER, -1), right_matrix(COLS_INNER, -1),
         left_matrix(ROWS_OUTER, 1), left_matrix(ROWS_INNER, 1),
         left_matrix(COLS_OUTER, 1), right_matrix(COLS_INNER, 1),
     )
     block = pltpu.VMEM((n, 2 * rows, LANES), BF16)
     floats = pltpu.VMEM((n * 2 * rows, LANES), F32)
     dma = pltpu.SemaphoreType.DMA
-    anywhere = pl.BlockSpec(memory_space=pl.ANY)
+    hbm = pl.BlockSpec(memory_space=pltpu.HBM)
     vmem = pl.BlockSpec(memory_space=pltpu.VMEM)
     spectrum_out, smoothed = pl.pallas_call(
         functools.partial(kernel, n, rows, "fft"),
         out_shape=(
             jax.ShapeDtypeStruct(spectrum_in.shape, BF16),
-            jax.ShapeDtypeStruct((rows, groups * n), F32),
+            jax.ShapeDtypeStruct((rows * groups * n // LANES, LANES), F32),
         ),
-        in_specs=[pl.BlockSpec(memory_space=pltpu.SMEM), anywhere, anywhere] + [vmem] * 8,
+        in_specs=[pl.BlockSpec(memory_space=pltpu.SMEM)] + [hbm] * 10,
         out_specs=(vmem, vmem),
-        scratch_shapes=[
-            pltpu.VMEM(spectrum_in.shape, BF16), block, block, block, block, block, floats, floats,
+        scratch_shapes=[pltpu.VMEM(m.shape, BF16) for m in matrices] + [
+            pltpu.VMEM(spectrum_in.shape, BF16), pltpu.VMEM((n, rows, 2, LANES), BF16), block, block, block, block, floats, floats,
             pltpu.VMEM((chips, groups, LANES), BF16), pltpu.VMEM((chips, groups, LANES), BF16),
             pltpu.VMEM((chips, groups, LANES), BF16), pltpu.VMEM((2, HALF_WIDTH, LANES), BF16),
             pltpu.VMEM((HALF_WIDTH, LANES), BF16), pltpu.VMEM((groups * n + 2 * HALF_WIDTH, LANES), F32),
             pltpu.VMEM((LANES, groups * n), F32),
             pltpu.VMEM((COLS_OUTER, LANES), F32), pltpu.VMEM((COLS_OUTER, LANES), F32),
-            dma((n,)), dma((n,)), dma((n,)), dma((n,)), dma((n,)), dma((n,)), dma((chips,)), dma((chips,)), dma((6,)),
+            dma((n,)), dma((n,)), dma((n,)), dma((n,)), dma((len(BATCHES) * n,)), dma((len(BATCHES) * n,)), dma((chips,)), dma((chips,)), dma((6,)), dma((8,)),
+            pltpu.SemaphoreType.REGULAR((2,)),
         ],
         compiler_params=pltpu.CompilerParams(
-            collective_id=0, has_side_effects=True, vmem_limit_bytes=60 * 2**20
+            collective_id=0, has_side_effects=True, vmem_limit_bytes=36 * 2**20
         ),
         name="dedisperse",
-    )(dm_index, blocks, spectrum_in, *matrices)
+    )(dm_index, *(pltpu.with_memory_space_constraint(a, pltpu.HBM) for a in (blocks, spectrum_in, *matrices)))
     return spectrum_out, smoothed.reshape(1, -1)
 
 

time: 634 us -> 586 us (0.924)
  Pallas kernels: 624 us -> 582 us
  local copies, waits for them, and re-layouts: 9.32 us -> 1.98 us
    pallas_call x1, Pallas kernels: 624 us -> 582 us  [on_device(): pl.pallas_call(functools.partial(kernel, n, rows, 'fft'), out_shape=(jax....]
where the time goes in v2:
time: 586 us
  Pallas kernels  582 us (99%)
    pallas_call x1, Pallas kernels, on_device(): pl.pallas_call(functools.partial(kernel, n, rows, 'fft'), out_shape=(jax....  582 us

profile of v2, /device:TPU:46, one launch (start us, length us, event | category | flops | bytes accessed | tf_op | source)
XLA Modules:
  0.0 585.6 jit_solution(5553709855139082772)
XLA Ops:
  1.3 582.3 %dedisperse.1 = (bf16[2,64,8192]{2,1,0:T(8,128)(2,1)S(1)}, f32[256,128]{1,0:T(8,128)S(1)}) custom-call(s32[1]{0:T(128)S(6)} %copy.15.dm_ref, bf16[64,64,2,128]{3,2,1,0:T(2,128)(2,1)} %bitcast.5, bf16[2,64,8192]{2,1,0:T(8,128)(2,1)} %spec.1, bf16[64,64]{1,0:T(8,128)(2,1)} %constant.12.clone.h1f, bf16[256,256]{1,0:T(8,128)(2,1)} %constant.13.clone.h2f.h4i, ...), custom_call_target="tpu_custom_call" | custom-call | tf_op jit(solution)/shard_map/dedisperse/pallas_call | solution.py:426
  583.6 1.3 copy.16
  584.9 0.7 copy.17

commit v3 on v2

--- a/solution.py
+++ b/solution.py
@@ -83,7 +83,7 @@
     dm_ref, xb, spec, h1f, h2f, h3f, h4f, h1i, h2i, h3i, h4i,
     out_ref, smooth_ref,
     m1f, m2f, m3f, m4f, m1i, m2i, m3i, m4i, spec_v, r1, r2, r3, s2, s3, fa, fb, sd, ra, rb, tb, halo, tpad, sm, twc, tws,
-    send1, recv1, send2, recv2, send3, recv3, send_d, recv_d, misc, loaded, ready,
+    sent, got, misc, loaded, ready,
 ):
     me = lax.axis_index(axis)
     chips = n // 2
@@ -105,7 +105,10 @@
 
     barrier = pltpu.get_barrier_semaphore()
 
-    near, middle = 2 * (chips - 1 - chips // 4), 2 * (chips - 1 - chips // 2)
+    def within(reach):
+        return 2 * max(chips - 1 - 2 * reach, 0)
+
+    near = within(1)
 
     @pl.loop(near, n - 1)
     def _(i):
@@ -119,9 +122,18 @@
             device_id={axis: target}, device_id_type=MESH,
         )
 
+    def whole(ref, number):
+        return remote(ref, ref, sent.at[number], got.at[number], 2 * z + 1 - core)
+
+    others = pl.ds(0, n - 1)
+
+    def rows_of(batch):
+        first_group, count = BATCHES[batch]
+        return r3.at[others, pl.ds(16 * first_group, 16 * count)]
+
     def first(i):
         x = peer(i)
-        return remote(xb.at[:, x], r1.at[me], send1.at[i], recv1.at[i], x)
+        return remote(xb.at[:, x], r1.at[me], sent.at[0], got.at[0], x)
 
     def send_first(start, stop):
         @pl.loop(start, stop)
@@ -129,12 +141,13 @@
             first(i).start()
 
     send_first(near, n - 1)
-    for level, (reach, start, stop) in enumerate(((chips // 8, middle, near), (chips // 4, 0, middle))):
+    for level in range(int(math.log2(chips)) - 1):
+        reach = 2**level
         for side in (reach, chips - reach):
             target = 2 * lax.rem(z + side, chips) + core
             pl.semaphore_signal(ready.at[level], inc=1, device_id={axis: target}, device_id_type=MESH)
         pl.semaphore_wait(ready.at[level], 2)
-        send_first(start, stop)
+        send_first(within(2 * reach), within(reach))
 
     m_iota = iota((rows, LANES), 0)
     lane = iota((rows, LANES), 1)
@@ -176,7 +189,7 @@
 
     def second(i):
         x = peer(i)
-        return remote(s2.at[x], r2.at[me], send2.at[i], recv2.at[i], x)
+        return remote(s2.at[x], r2.at[me], sent.at[1], got.at[1], x)
 
     @pl.loop(0, n - 1)
     def _(i):
@@ -188,9 +201,7 @@
 
     load_own.wait()
 
-    @pl.loop(0, n - 1)
-    def _(i):
-        first(i).wait_recv()
+    whole(r1.at[others], 0).wait_recv()
 
     @pl.loop(0, n)
     def _(d):
@@ -221,8 +232,7 @@
         x = peer(i)
         first_group, count = BATCHES[batch]
         at = pl.ds(16 * first_group, 16 * count)
-        step = batch * n + i
-        return remote(s3.at[x, at], r3.at[me, at], send3.at[step], recv3.at[step], x)
+        return remote(s3.at[x, at], r3.at[me, at], sent.at[3 + batch], got.at[3 + batch], x)
 
     @pl.loop(0, chips)
     def _(i):
@@ -247,9 +257,7 @@
 
     r3[me] = s3[me]
 
-    @pl.loop(0, n - 1)
-    def _(i):
-        second(i).wait_recv()
+    whole(r2.at[others], 1).wait_recv()
 
     @pl.loop(0, chips)
     def _(p):
@@ -287,7 +295,7 @@
 
     def detected(i):
         x = lax.rem(z + order(i, chips), chips)
-        return remote(sd.at[x], ra.at[z], send_d.at[i], recv_d.at[i], 2 * x + core)
+        return remote(sd.at[x], ra.at[z], sent.at[2], got.at[2], 2 * x + core)
 
     @pl.loop(0, chips - 1)
     def _(i):
@@ -308,10 +316,7 @@
     tws[...] = si
 
     def columns_of(batch):
-        @pl.loop(0, n - 1)
-        def _(i):
-            third(batch, i).wait_recv()
-
+        whole(rows_of(batch), 3 + batch).wait_recv()
         first_group, count = BATCHES[batch]
 
         @pl.loop(first_group, first_group + count)
@@ -338,9 +343,7 @@
 
     columns_of(0)
 
-    @pl.loop(0, chips - 1)
-    def _(i):
-        detected(i).wait_recv()
+    whole(ra.at[pl.ds(0, chips - 1)], 2).wait_recv()
 
     swap = remote(ra, rb, misc.at[2], misc.at[3], 2 * z + 1 - core)
     swap.start()
@@ -364,12 +367,12 @@
     columns_of(1)
     edge.wait_recv()
     inside = ((z > 0) | (core == 1)) & ((z < chips - 1) | (core == 0))
-    got = jnp.where(inside, halo[...].astype(F32), 0.0)
+    aside_rows = jnp.where(inside, halo[...].astype(F32), 0.0)
     edge_lane = iota((HALF_WIDTH, LANES), 1)
-    above = jnp.where(edge_lane == 0, pltpu.roll(got, 1, 1), pltpu.roll(tpad[series : series + HALF_WIDTH, :], 1, 1))
+    above = jnp.where(edge_lane == 0, pltpu.roll(aside_rows, 1, 1), pltpu.roll(tpad[series : series + HALF_WIDTH, :], 1, 1))
     below = jnp.where(
         edge_lane == LANES - 1,
-        pltpu.roll(got, LANES - 1, 1),
+        pltpu.roll(aside_rows, LANES - 1, 1),
         pltpu.roll(tpad[HALF_WIDTH : 2 * HALF_WIDTH, :], LANES - 1, 1),
     )
     tpad[:HALF_WIDTH, :] = above
@@ -391,17 +394,11 @@
     for batch in range(2, len(BATCHES)):
         columns_of(batch)
 
-    @pl.loop(0, n - 1)
-    def _(i):
-        first(i).wait_send()
-        second(i).wait_send()
-        for batch in range(len(BATCHES)):
-            third(batch, i).wait_send()
-
-    @pl.loop(0, chips - 1)
-    def _(i):
-        detected(i).wait_send()
-
+    whole(r1.at[others], 0).wait_send()
+    whole(r2.at[others], 1).wait_send()
+    whole(ra.at[pl.ds(0, chips - 1)], 2).wait_send()
+    for batch in range(len(BATCHES)):
+        whole(rows_of(batch), 3 + batch).wait_send()
     swap.wait_send()
     edge.wait_send()
 
@@ -438,8 +435,8 @@
             pltpu.VMEM((HALF_WIDTH, LANES), BF16), pltpu.VMEM((groups * n + 2 * HALF_WIDTH, LANES), F32),
             pltpu.VMEM((LANES, groups * n), F32),
             pltpu.VMEM((COLS_OUTER, LANES), F32), pltpu.VMEM((COLS_OUTER, LANES), F32),
-            dma((n,)), dma((n,)), dma((n,)), dma((n,)), dma((len(BATCHES) * n,)), dma((len(BATCHES) * n,)), dma((chips,)), dma((chips,)), dma((6,)), dma((8,)),
-            pltpu.SemaphoreType.REGULAR((2,)),
+            dma((3 + len(BATCHES),)), dma((3 + len(BATCHES),)), dma((6,)), dma((8,)),
+            pltpu.SemaphoreType.REGULAR((int(math.log2(chips)) - 1,)),
         ],
         compiler_params=pltpu.CompilerParams(
             collective_id=0, has_side_effects=True, vmem_limit_bytes=36 * 2**20

time: 586 us -> 577 us (0.985)
  Pallas kernels: 582 us -> 573 us
    pallas_call x1, Pallas kernels: 582 us -> 573 us  [on_device(): pl.pallas_call(functools.partial(kernel, n, rows, 'fft'), out_shape=(jax....]
where the time goes in v3:
time: 577 us; the launch traced here: 576 us
  Pallas kernels  573 us (99%)
    pallas_call x1, Pallas kernels, on_device(): pl.pallas_call(functools.partial(kernel, n, rows, 'fft'), out_shape=(jax....  573 us

profile of v3, /device:TPU:46, one launch (start us, length us, event | category | flops | bytes accessed | tf_op | source)
XLA Modules:
  0.0 576.0 jit_solution(13986758546235474163)
XLA Ops:
  1.3 572.8 %dedisperse.1 = (bf16[2,64,8192]{2,1,0:T(8,128)(2,1)S(1)}, f32[256,128]{1,0:T(8,128)S(1)}) custom-call(s32[1]{0:T(128)S(6)} %copy.15.dm_ref, bf16[64,64,2,128]{3,2,1,0:T(2,128)(2,1)} %bitcast.5, bf16[2,64,8192]{2,1,0:T(8,128)(2,1)} %spec.1, bf16[64,64]{1,0:T(8,128)(2,1)} %constant.12.clone.h1f, bf16[256,256]{1,0:T(8,128)(2,1)} %constant.13.clone.h2f.h4i, ...), custom_call_target="tpu_custom_call" | custom-call | tf_op jit(solution)/shard_map/dedisperse/pallas_call | solution.py:423
  574.1 1.3 copy.16
  575.4 0.7 copy.17

commit v4 on v3

--- a/solution.py
+++ b/solution.py
@@ -78,10 +78,47 @@
     return odd * lax.div(t + 1, 2) + (1 - odd) * (chips - lax.div(t, 2))
 
 
+def columns(blocks, n, m3f, m4f, co, si, fa, fb):
+    for d in range(n):
+        fa[16 * d : 16 * (d + 1), :] = blocks(d).astype(F32)
+    for m in range(8):
+        x = jnp.concatenate([fa[pl.ds(8 * part + m, n, stride=16), :] for part in range(2)], axis=0)
+        v = dot(m3f[...], x.astype(BF16))
+        vr, vi = v[:COLS_OUTER], v[COLS_OUTER:]
+        fb[pl.ds(m, COLS_OUTER, stride=8), :] = vr * co + vi * si
+        fb[pl.ds(8 * COLS_OUTER + m, COLS_OUTER, stride=8), :] = vi * co - vr * si
+    half = 8 * COLS_OUTER
+    a = jnp.concatenate([fb[:half, :].astype(BF16), fb[half : 2 * half, :].astype(BF16)], axis=1)
+    return dot(a, m4f[...])
+
+
+def block_of(v, c, part):
+    return v[8 * c : 8 * (c + 1), part * LANES : (part + 1) * LANES].astype(BF16)
+
+
+def last_group(n, done, smooth, last, m3f, m4f, out, smooth_out, fa, fb, staged, sems):
+    ready = BATCHES[-1][0] * 8
+    copies = [
+        pltpu.make_async_copy(done.at[:, pl.ds(0, ready)], out.at[:, pl.ds(0, ready)], sems.at[0]),
+        pltpu.make_async_copy(smooth, smooth_out, sems.at[1]),
+    ]
+    for copy in copies:
+        copy.start()
+    co, si = unit(iota((COLS_OUTER, LANES), 0) * iota((COLS_OUTER, LANES), 1), COLUMN_LENGTH)
+    v = columns(lambda d: last[16 * d : 16 * (d + 1), :], n, m3f, m4f, co, si, fa, fb)
+    for c in range(COLS_OUTER):
+        for part in range(2):
+            staged[part, :, c * LANES : (c + 1) * LANES] = block_of(v, c, part)
+    copies.append(pltpu.make_async_copy(staged, out.at[:, pl.ds(ready, 8)], sems.at[2]))
+    copies[-1].start()
+    for copy in copies:
+        copy.wait()
+
+
 def kernel(
     n, rows, axis,
     dm_ref, xb, spec, h1f, h2f, h3f, h4f, h1i, h2i, h3i, h4i,
-    out_ref, smooth_ref,
+    out_ref, smooth_ref, last, m3_out, m4_out,
     m1f, m2f, m3f, m4f, m1i, m2i, m3i, m4i, spec_v, r1, r2, r3, s2, s3, fa, fb, sd, ra, rb, tb, halo, tpad, sm, twc, tws,
     sent, got, misc, loaded, ready,
 ):
@@ -156,6 +193,8 @@
     row_turns = (steps * freq_row * freq_row).astype(F32) * (2.0 ** -33)
     for load in loads:
         load.wait()
+    m3_out[...] = m3f[...]
+    m4_out[...] = m4f[...]
 
     @pl.loop(0, COLS_OUTER)
     def _(c):
@@ -322,24 +361,11 @@
         @pl.loop(first_group, first_group + count)
         def _(g):
             at = pl.ds(pl.multiple_of(16 * g, 16), 16)
-            for d in range(n):
-                fa[16 * d : 16 * (d + 1), :] = r3[d, at, :].astype(F32)
-            co, si = twc[...], tws[...]
-            for m in range(8):
-                x = jnp.concatenate([fa[pl.ds(8 * part + m, n, stride=16), :] for part in range(2)], axis=0)
-                v = dot(m3f[...], x.astype(BF16))
-                vr, vi = v[:COLS_OUTER], v[COLS_OUTER:]
-                fb[pl.ds(m, COLS_OUTER, stride=8), :] = vr * co + vi * si
-                fb[pl.ds(8 * COLS_OUTER + m, COLS_OUTER, stride=8), :] = vi * co - vr * si
-            a = jnp.concatenate(
-                [fb[: 8 * COLS_OUTER, :].astype(BF16), fb[8 * COLS_OUTER : 16 * COLS_OUTER, :].astype(BF16)], axis=1
-            )
-            v = dot(a, m4f[...])
+            v = columns(lambda d: r3[d, at, :], n, m3f, m4f, twc[...], tws[...], fa, fb)
             at = pl.ds(pl.multiple_of(8 * g, 8), 8)
             for c in range(COLS_OUTER):
                 for part in range(2):
-                    block = v[8 * c : 8 * (c + 1), part * LANES : (part + 1) * LANES]
-                    out_ref[part, at, c * LANES : (c + 1) * LANES] = block.astype(BF16)
+                    out_ref[part, at, c * LANES : (c + 1) * LANES] = block_of(v, c, part)
 
     columns_of(0)
 
@@ -391,8 +417,14 @@
     for i in range(series // LANES):
         smooth_ref[pl.ds(i, rows, stride=series // LANES), :] = sm[own_rows, i * LANES : (i + 1) * LANES]
 
-    for batch in range(2, len(BATCHES)):
+    for batch in range(2, len(BATCHES) - 1):
         columns_of(batch)
+
+    final = len(BATCHES) - 1
+    whole(rows_of(final), 3 + final).wait_recv()
+    for d in range(n):
+        last[16 * d : 16 * (d + 1), :] = r3[d, 16 * BATCHES[final][0] : 16 * (BATCHES[final][0] + 1), :]
+
 
     whole(r1.at[others], 0).wait_send()
     whole(r2.at[others], 1).wait_send()
@@ -420,14 +452,17 @@
     dma = pltpu.SemaphoreType.DMA
     hbm = pl.BlockSpec(memory_space=pltpu.HBM)
     vmem = pl.BlockSpec(memory_space=pltpu.VMEM)
-    spectrum_out, smoothed = pl.pallas_call(
+    parts = pl.pallas_call(
         functools.partial(kernel, n, rows, "fft"),
         out_shape=(
             jax.ShapeDtypeStruct(spectrum_in.shape, BF16),
             jax.ShapeDtypeStruct((rows * groups * n // LANES, LANES), F32),
+            jax.ShapeDtypeStruct((16 * n, LANES), BF16),
+            jax.ShapeDtypeStruct(matrices[2].shape, BF16),
+            jax.ShapeDtypeStruct(matrices[3].shape, BF16),
         ),
         in_specs=[pl.BlockSpec(memory_space=pltpu.SMEM)] + [hbm] * 10,
-        out_specs=(vmem, vmem),
+        out_specs=(vmem,) * 5,
         scratch_shapes=[pltpu.VMEM(m.shape, BF16) for m in matrices] + [
             pltpu.VMEM(spectrum_in.shape, BF16), pltpu.VMEM((n, rows, 2, LANES), BF16), block, block, block, block, floats, floats,
             pltpu.VMEM((chips, groups, LANES), BF16), pltpu.VMEM((chips, groups, LANES), BF16),
@@ -443,6 +478,15 @@
         ),
         name="dedisperse",
     )(dm_index, *(pltpu.with_memory_space_constraint(a, pltpu.HBM) for a in (blocks, spectrum_in, *matrices)))
+    floats = pltpu.VMEM((16 * n, LANES), F32)
+    spectrum_out, smoothed = pl.pallas_call(
+        functools.partial(last_group, n),
+        out_shape=tuple(jax.ShapeDtypeStruct(a.shape, a.dtype) for a in parts[:2]),
+        in_specs=[vmem] * 5,
+        out_specs=(hbm, hbm),
+        scratch_shapes=[floats, floats, pltpu.VMEM((2, 8, COLUMN_LENGTH), BF16), dma((3,))],
+        name="last_group",
+    )(*(pltpu.with_memory_space_constraint(a, pltpu.VMEM) for a in parts))
     return spectrum_out, smoothed.reshape(1, -1)
 
 

time: 577 us -> 576 us (level)
  no operation moved by 1% of the time
where the time goes in v4:
time: 576 us; the launch traced here: 575 us
  Pallas kernels  574 us (100%)
    pallas_call x1, Pallas kernels, on_device(): pl.pallas_call(functools.partial(kernel, n, rows, 'fft'), out_shape=(jax....  572 us

profile of v4, /device:TPU:46, one launch (start us, length us, event | category | flops | bytes accessed | tf_op | source)
XLA Modules:
  0.0 575.0 jit_solution(3495643681802000996)
XLA Ops:
  1.3 572.2 %dedisperse.1 = (bf16[2,64,8192]{2,1,0:T(8,128)(2,1)S(1)}, f32[256,128]{1,0:T(8,128)S(1)}, bf16[1024,128]{1,0:T(8,128)(2,1)S(1)}, bf16[128,128]{1,0:T(8,128)(2,1)S(1)}, bf16[256,256]{1,0:T(8,128)(2,1)S(1)}) custom-call(s32[1]{0:T(128)S(6)} %copy.13.dm_ref, bf16[64,64,2,128]{3,2,1,0:T(2,128)(2,1)} %bitcast.4, bf16[2,64,8192]{2,1,0:T(8,128)(2,1)} %spec.1, ...), custom_call_target="tpu_custom_call" | custom-call | tf_op jit(solution)/shard_map/dedisperse/pallas_call | solution.py:455
  573.5 1.5 last_group.1
